TPU v7x, 32 devices: a 4x2x2 block of a 4x4x8 slice. The times are simulated.
32 devices in a mesh: dp: 4 (over y, z), cp: 8 (over x, core).
Axes of the slice: x: 4, y: 2, z: 2, core: 2. Of those that a mesh axis runs over, the one named last changes fastest.
The devices are a block of a 4x4x8 slice.
Arguments:
- latent: bfloat16 [64, 6, 96, 512], P(('dp', 'cp')), parts along dimension 0
- conv_kernels: bfloat16 [4, 3, 3, 3, 512, 512], replicated
- conv_biases: float32 [4, 512], replicated
- gn_gammas: float32 [4, 512], replicated
- gn_betas: float32 [4, 512], replicated
Outputs:
- output: bfloat16 [64, 6, 96, 512], P(('dp', 'cp')), parts along dimension 0
There are 4 independent parts. A program takes and returns all parts, laid end to end along the dimension named above; an argument that names none is the same for every part.
All inputs are finite; a program needn't handle non-finite values.
Results may differ from a plain program's by a relative error of at most 0.0124199.
Values are sent between devices in bfloat16 or wider.
A program may use at most 768 MiB of HBM per device.

v0:
```python
import jax
import jax.numpy as jnp
from jax import lax
from jax.sharding import PartitionSpec as P

GROUPS = 32
NORM_EPS = 1e-6


def group_sums(hidden):
    n_frames, n_rows, n_cols, n_chans = hidden.shape
    grouped = hidden.astype(jnp.float32).reshape(n_frames, n_rows, n_cols, GROUPS, n_chans // GROUPS)
    return jnp.stack([jnp.sum(grouped, axis=(0, 1, 2, 4)), jnp.sum(grouped * grouped, axis=(0, 1, 2, 4))])


def norm_act(hidden, grp_sums, elem_count, gn_gamma, gn_beta):
    grp_mean = grp_sums[0] / elem_count
    grp_var = grp_sums[1] / elem_count - grp_mean * grp_mean
    group_width = hidden.shape[-1] // GROUPS
    chan_scale = jnp.repeat(lax.rsqrt(grp_var + NORM_EPS), group_width) * gn_gamma
    chan_shift = gn_beta - jnp.repeat(grp_mean, group_width) * chan_scale
    normed = (hidden.astype(jnp.float32) * chan_scale + chan_shift).astype(jnp.bfloat16)
    return jax.nn.silu(normed.astype(jnp.float32)).astype(jnp.bfloat16)


def conv_frames(padded, kernel, conv_bias):
    result = lax.conv_general_dilated(padded[None], kernel, window_strides=(1, 1, 1), padding=((0, 0), (1, 1), (1, 1)), dimension_numbers=("NDHWC", "DHWIO", "NDHWC"), preferred_element_type=jnp.float32)[0]
    return (result + conv_bias).astype(jnp.bfloat16)


def solution(mesh):
    n_time = mesh.shape["cp"]
    next_perm = [(src, src + 1) for src in range(n_time - 1)]
    frame_spec = P(("dp", "cp"))

    def local_fn(latent, conv_kernels, conv_biases, gn_gammas, gn_betas):
        n_frames, n_rows, n_cols, n_chans = latent.shape
        my_rank = lax.axis_index("cp")
        elem_count = n_time * n_frames * n_rows * n_cols * (n_chans // GROUPS)

        def gn_step(hidden, layer_idx):
            grp_sums = lax.psum(group_sums(hidden), "cp")
            return norm_act(hidden, grp_sums, elem_count, gn_gammas[layer_idx], gn_betas[layer_idx])

        def conv_step(act_in, layer_idx):
            from_prev = lax.ppermute(act_in[n_frames - 2:], "cp", next_perm)
            own_first = jnp.concatenate([act_in[:1], act_in[:1]], axis=0)
            halo_frames = jnp.where(my_rank == 0, own_first, from_prev)
            return conv_frames(jnp.concatenate([halo_frames, act_in], axis=0), conv_kernels[layer_idx], conv_biases[layer_idx])

        hidden = latent
        for block_idx in range(2):
            first_layer = 2 * block_idx
            inner = conv_step(gn_step(hidden, first_layer), first_layer)
            inner = conv_step(gn_step(inner, first_layer + 1), first_layer + 1)
            hidden = (hidden.astype(jnp.float32) + inner.astype(jnp.float32)).astype(jnp.bfloat16)
        return hidden

    return jax.shard_map(local_fn, mesh=mesh, in_specs=(frame_spec, P(), P(), P(), P()), out_specs=frame_spec, check_vma=False)
```

profile of v0, /device:TPU:81, one launch (start us, length us, event | category | flops | bytes accessed | tf_op | source)
XLA Modules:
  0.0 254.4 jit_solution(3934144692596810975)
XLA Ops:
  0.0 1.7 convert_reduce_fusion.1
  2.1 13.9 %psum.28 = f32[2,32]{1,0:T(2,128)S(1)} all-reduce(f32[2,32]{1,0:T(2,128)S(1)} %pad_maximum_fusion), channel_id=1, replica_groups=mesh['dp'=4,'cp'=8] {'cp'}, use_global_device_ids=true, to_apply=%region_4.5 | all-reduce | flops 64 | bytes 512 | tf_op jit(solution)/shard_map/psum | solution.py:42
  15.9 0.9 fusion.124
  18.0 1.9 fusion.49
  19.9 2.8 %collective-permute-start = (bf16[2,6,96,512]{3,2,1,0:T(8,128)(2,1)S(1)}, bf16[2,6,96,512]{3,2,1,0:T(8,128)(2,1)S(1)}, u32[]{:S(2)}, u32[]{:S(2)}) collective-permute-start(bf16[2,6,96,512]{3,2,1,0:T(8,128)(2,1)S(1)} %fusion.49), channel_id=1, source_target_pairs={{0,1},{1,2},{2,3},{3,4},{4,5},{5,6},{6,7},{8,9},{9,10},{10,11},{11... | collective-permute-start | bytes 3538952 | tf_op jit(solution)/shard_map/ppermute | solution.py:46
  23.4 12.4 %collective-permute-done = bf16[2,6,96,512]{3,2,1,0:T(8,128)(2,1)S(1)} collective-permute-done((bf16[2,6,96,512]{3,2,1,0:T(8,128)(2,1)S(1)}, bf16[2,6,96,512]{3,2,1,0:T(8,128)(2,1)S(1)}, u32[]{:S(2)}, u32[]{:S(2)}) %collective-permute-start) | collective-permute-done | bytes 1179680 | tf_op jit(solution)/shard_map/ppermute | solution.py:46
  36.2 1.8 copy.44
  38.0 1.0 pad.clone
  39.7 25.2 %fusion.40 = (f32[512]{0:T(512)S(1)}, f32[512]{0:T(512)S(1)}, f32[2,6,8,13,512]{4,2,3,1,0:T(8,128)S(1)}) fusion(pred[8,13]{0,1:T(8,128)(4,1)S(1)} %copy-done.3, f32[512]{0:T(512)S(1)} %bitcast.169, bf16[4,3,3,3,512,512]{5,4,3,2,1,0:T(8,128)(2,1)} %param.6, bf16[4,6,1,7,2,512]{5,3,4,1,0,2:T(8,128)(2,1)S(1)} %slice.125, ...), kind=kOutput, calls=%fused_computation.57 | convolution fusion | flops 15718072320 | bytes 19617896 | tf_op jit(solution)/shard_map/conv_general_dilated | solution.py:27
  65.3 12.0 %psum.29 = f32[2,32]{1,0:T(2,128)S(1)} all-reduce(f32[2,32]{1,0:T(2,128)S(1)} %pad_maximum_fusion.1), channel_id=1, replica_groups=mesh['dp'=4,'cp'=8] {'cp'}, use_global_device_ids=true, to_apply=%region_9.10 | all-reduce | flops 64 | bytes 512 | tf_op jit(solution)/shard_map/psum | solution.py:42
  77.6 2.0 copy.23
  81.2 2.7 %collective-permute-start.1 = (bf16[2,6,96,512]{3,2,1,0:T(8,128)(2,1)S(1)}, bf16[2,6,96,512]{3,2,1,0:T(8,128)(2,1)S(1)}, u32[]{:S(2)}, u32[]{:S(2)}) collective-permute-start(bf16[2,6,96,512]{3,2,1,0:T(8,128)(2,1)S(1)} %fusion.53), channel_id=1, source_target_pairs={{0,1},{1,2},{2,3},{3,4},{4,5},{5,6},{6,7},{8,9},{9,10},{10,11},{11... | collective-permute-start | bytes 3538952 | tf_op jit(solution)/shard_map/ppermute | solution.py:46
  84.0 13.0 %collective-permute-done.1 = bf16[2,6,96,512]{3,2,1,0:T(8,128)(2,1)S(1)} collective-permute-done((bf16[2,6,96,512]{3,2,1,0:T(8,128)(2,1)S(1)}, bf16[2,6,96,512]{3,2,1,0:T(8,128)(2,1)S(1)}, u32[]{:S(2)}, u32[]{:S(2)}) %collective-permute-start.1) | collective-permute-done | bytes 1179680 | tf_op jit(solution)/shard_map/ppermute | solution.py:46
  97.4 1.8 copy.45
  99.2 1.0 pad.2.clone
  100.8 25.5 %fusion.87 = f32[2,6,8,13,512]{4,2,3,1,0:T(8,128)S(1)} fusion(bf16[4,3,3,3,512,512]{5,4,3,2,1,0:T(8,128)(2,1)} %param.6, bf16[4,6,1,7,2,512]{5,3,4,1,0,2:T(8,128)(2,1)S(1)} %slice.128, bf16[4,6,1,8,13,512]{5,3,4,1,0,2:T(8,128)(2,1)S(1)} %copy.27, pred[8,13]{0,1:T(8,128)(4,1)S(1)} %copy-done.3), kind=kOutput, calls=%fused_computation.112 | convolution fusion | flops 15712960512 | bytes 19611752 | tf_op jit(solution)/shard_map/conv_general_dilated | solution.py:27
  126.3 2.0 copy.28
  130.6 11.8 %psum.30 = f32[2,32]{1,0:T(2,128)S(1)} all-reduce(f32[2,32]{1,0:T(2,128)S(1)} %pad_maximum_fusion.2), channel_id=1, replica_groups=mesh['dp'=4,'cp'=8] {'cp'}, use_global_device_ids=true, to_apply=%region_14.15 | all-reduce | flops 64 | bytes 512 | tf_op jit(solution)/shard_map/psum | solution.py:42
  143.4 2.7 %collective-permute-start.2 = (bf16[2,6,96,512]{3,2,1,0:T(8,128)(2,1)S(1)}, bf16[2,6,96,512]{3,2,1,0:T(8,128)(2,1)S(1)}, u32[]{:S(2)}, u32[]{:S(2)}) collective-permute-start(bf16[2,6,96,512]{3,2,1,0:T(8,128)(2,1)S(1)} %fusion.57), channel_id=1, source_target_pairs={{0,1},{1,2},{2,3},{3,4},{4,5},{5,6},{6,7},{8,9},{9,10},{10,11},{11... | collective-permute-start | bytes 3538952 | tf_op jit(solution)/shard_map/ppermute | solution.py:46
  146.2 13.1 %collective-permute-done.2 = bf16[2,6,96,512]{3,2,1,0:T(8,128)(2,1)S(1)} collective-permute-done((bf16[2,6,96,512]{3,2,1,0:T(8,128)(2,1)S(1)}, bf16[2,6,96,512]{3,2,1,0:T(8,128)(2,1)S(1)}, u32[]{:S(2)}, u32[]{:S(2)}) %collective-permute-start.2) | collective-permute-done | bytes 1179680 | tf_op jit(solution)/shard_map/ppermute | solution.py:46
  159.6 1.8 copy.46
  161.4 1.0 pad.4.clone
  163.0 23.5 %fusion.43 = (f32[512]{0:T(512)S(1)}, f32[512]{0:T(512)S(1)}, f32[2,6,8,13,512]{4,2,3,1,0:T(8,128)}) fusion(pred[8,13]{0,1:T(8,128)(4,1)S(1)} %copy-done.3, f32[512]{0:T(512)S(1)} %bitcast.167, bf16[4,3,3,3,512,512]{5,4,3,2,1,0:T(8,128)(2,1)} %param.6, bf16[4,6,1,7,2,512]{5,3,4,1,0,2:T(8,128)(2,1)S(1)} %slice.131, bf16[4,6,1,8,13,512]{5,3,4,1,0,2:T(8,128)(2,1)S(1)} %copy.32), kind=kOutput, calls=%fused_computation.60 | convolution fusion | flops 15718072320 | bytes 19617896 | tf_op jit(solution)/shard_map/conv_general_dilated | solution.py:27
  186.9 12.0 %psum.31 = f32[2,32]{1,0:T(2,128)S(1)} all-reduce(f32[2,32]{1,0:T(2,128)S(1)} %pad_maximum_fusion.3), channel_id=1, replica_groups=mesh['dp'=4,'cp'=8] {'cp'}, use_global_device_ids=true, to_apply=%region_19.20 | all-reduce | flops 64 | bytes 512 | tf_op jit(solution)/shard_map/psum | solution.py:42
  199.2 3.7 %copy.33 = f32[2,6,8,13,512]{4,0,3,2,1:T(2,128)S(1)} copy(f32[2,6,8,13,512]{4,2,3,1,0:T(8,128)} %get-tuple-element.35) | data formatting | bytes 5111808 | tf_op jit(solution)/shard_map/conv_general_dilated | solution.py:27
  204.5 2.7 %collective-permute-start.3 = (bf16[2,6,96,512]{3,2,1,0:T(8,128)(2,1)S(1)}, bf16[2,6,96,512]{3,2,1,0:T(8,128)(2,1)S(1)}, u32[]{:S(2)}, u32[]{:S(2)}) collective-permute-start(bf16[2,6,96,512]{3,2,1,0:T(8,128)(2,1)S(1)} %fusion.61), channel_id=1, source_target_pairs={{0,1},{1,2},{2,3},{3,4},{4,5},{5,6},{6,7},{8,9},{9,10},{10,11},{11... | collective-permute-start | bytes 3538952 | tf_op jit(solution)/shard_map/ppermute | solution.py:46
  207.3 13.0 %collective-permute-done.3 = bf16[2,6,96,512]{3,2,1,0:T(8,128)(2,1)S(1)} collective-permute-done((bf16[2,6,96,512]{3,2,1,0:T(8,128)(2,1)S(1)}, bf16[2,6,96,512]{3,2,1,0:T(8,128)(2,1)S(1)}, u32[]{:S(2)}, u32[]{:S(2)}) %collective-permute-start.3) | collective-permute-done | bytes 1179680 | tf_op jit(solution)/shard_map/ppermute | solution.py:46
  220.8 1.8 copy.47
  222.6 1.0 pad.6.clone
  224.2 25.4 %fusion.97 = f32[2,6,8,13,512]{4,2,3,1,0:T(8,128)S(1)} fusion(bf16[4,3,3,3,512,512]{5,4,3,2,1,0:T(8,128)(2,1)} %param.6, bf16[4,6,1,7,2,512]{5,3,4,1,0,2:T(8,128)(2,1)S(1)} %slice.134, bf16[4,6,1,8,13,512]{5,3,4,1,0,2:T(8,128)(2,1)S(1)} %copy.37, pred[8,13]{0,1:T(8,128)(4,1)S(1)} %copy-done.3), kind=kOutput, calls=%fused_computation.114 | convolution fusion | flops 15712960512 | bytes 19611752 | tf_op jit(solution)/shard_map/conv_general_dilated | solution.py:27
  249.6 2.0 copy.38
  252.4 1.5 fusion.69
  (86 shorter events, 14.9 us)
Async XLA Ops:
  0.0 22.8 %copy-start.2 = (f32[4,512]{1,0:T(4,128)S(1)}, f32[4,512]{1,0:T(4,128)}, u32[]{:S(2)}) copy-start(f32[4,512]{1,0:T(4,128)} %param.7) | copy-start | bytes 24580
  19.9 15.9 %collective-permute-start = (bf16[2,6,96,512]{3,2,1,0:T(8,128)(2,1)S(1)}, bf16[2,6,96,512]{3,2,1,0:T(8,128)(2,1)S(1)}, u32[]{:S(2)}, u32[]{:S(2)}) collective-permute-start(bf16[2,6,96,512]{3,2,1,0:T(8,128)(2,1)S(1)} %fusion.49), channel_id=1, source_target_pairs={{0,1},{1,2},{2,3},{3,4},{4,5},{5,6},{6,7},{8,9},{9,10},{10,11},{11... | collective-permute-start | bytes 3538952 | tf_op jit(solution)/shard_map/ppermute | solution.py:46
  39.0 0.7 copy-start.3
  81.2 15.8 %collective-permute-start.1 = (bf16[2,6,96,512]{3,2,1,0:T(8,128)(2,1)S(1)}, bf16[2,6,96,512]{3,2,1,0:T(8,128)(2,1)S(1)}, u32[]{:S(2)}, u32[]{:S(2)}) collective-permute-start(bf16[2,6,96,512]{3,2,1,0:T(8,128)(2,1)S(1)} %fusion.53), channel_id=1, source_target_pairs={{0,1},{1,2},{2,3},{3,4},{4,5},{5,6},{6,7},{8,9},{9,10},{10,11},{11... | collective-permute-start | bytes 3538952 | tf_op jit(solution)/shard_map/ppermute | solution.py:46
  128.3 1.3 copy-start
  143.4 15.8 %collective-permute-start.2 = (bf16[2,6,96,512]{3,2,1,0:T(8,128)(2,1)S(1)}, bf16[2,6,96,512]{3,2,1,0:T(8,128)(2,1)S(1)}, u32[]{:S(2)}, u32[]{:S(2)}) collective-permute-start(bf16[2,6,96,512]{3,2,1,0:T(8,128)(2,1)S(1)} %fusion.57), channel_id=1, source_target_pairs={{0,1},{1,2},{2,3},{3,4},{4,5},{5,6},{6,7},{8,9},{9,10},{10,11},{11... | collective-permute-start | bytes 3538952 | tf_op jit(solution)/shard_map/ppermute | solution.py:46
  204.5 15.8 %collective-permute-start.3 = (bf16[2,6,96,512]{3,2,1,0:T(8,128)(2,1)S(1)}, bf16[2,6,96,512]{3,2,1,0:T(8,128)(2,1)S(1)}, u32[]{:S(2)}, u32[]{:S(2)}) collective-permute-start(bf16[2,6,96,512]{3,2,1,0:T(8,128)(2,1)S(1)} %fusion.61), channel_id=1, source_target_pairs={{0,1},{1,2},{2,3},{3,4},{4,5},{5,6},{6,7},{8,9},{9,10},{10,11},{11... | collective-permute-start | bytes 3538952 | tf_op jit(solution)/shard_map/ppermute | solution.py:46
  251.6 0.8 copy-start.1
where the time goes:
time: 259 us; the launch traced here: 254 us
  matrix products  99.5 us (38%)
  waiting for transfers between devices  51.6 us (20%)
  blocking collectives  49.7 us (19%)
  local copies, waits for them, and re-layouts  31.3 us (12%)
  starting transfers between devices  11 us (4%)
  other arithmetic  10.4 us (4%)
    conv_general_dilated x4, matrix products, conv_frames(): lax.conv_general_dilated(padded[None], kernel, window_strides=(1, 1, 1),...  99.5 us
    ppermute x4, waiting for transfers between devices, conv_step(): from_prev = lax.ppermute(act_in[n_frames - 2:], 'cp', next_perm)  51.6 us
    psum x4, blocking collectives, gn_step(): grp_sums = lax.psum(group_sums(hidden), 'cp')  49.7 us
    conv_general_dilated x16, local copies, waits for them, and re-layouts, conv_frames(): lax.conv_general_dilated(padded[None], kernel, window_strides=(1, 1, 1),...  15.3 us
    ppermute x4, starting transfers between devices, conv_step(): from_prev = lax.ppermute(act_in[n_frames - 2:], 'cp', next_perm)  11 us
    unnamed x12, local copies, waits for them, and re-layouts  7.82 us
  transfers between devices with their start and end apart: 4, of which 4 were waited for; matrix products, arithmetic and copies ran while one was open for 0% of the time, Pallas kernels for 0%

commit v1 on v0

v1 whole, which is shorter than its diff:
```python
import functools

import jax
import jax.numpy as jnp
from jax import lax
from jax.experimental import pallas as pl
from jax.experimental.pallas import tpu as pltpu
from jax.sharding import PartitionSpec as P

GROUPS = 32
NORM_EPS = 1e-6
N_LAYERS = 4
HALF = 256
SKEW = 1
MESH = pl.DeviceIdType.MESH


def interleave(long, short):
    if not short:
        return list(long)
    out, taken = [], 0
    for idx, job in enumerate(long):
        due = (idx * len(short)) // max(len(long), 1) + 1
        while taken < min(due, len(short)):
            out.append(short[taken])
            taken += 1
        out.append(job)
    return out + list(short[taken:])


def make_kernel(n_ranks, n_frames, n_rows, n_cols, n_chans):
    width = n_chans // GROUPS
    elem_count = float(n_ranks * n_frames * n_rows * n_cols * width)
    halves = n_chans // HALF

    def kernel(latent, weights, biases, gammas, betas, out, wbuf, act_l, act_c, act_r, raw, stat, sums, coef,
               w_sem, lat_sem, out_sem, halo_send, halo_recv, st_send, st_recv):
        acts = {-1: act_l, 0: act_c, 1: act_r}
        me = lax.axis_index("cp")
        is_first = me == 0
        has_next = me < n_ranks - 1

        def weight_copy(layer, slot, k):
            return pltpu.make_async_copy(weights.at[layer, pl.ds(9 * k, 9)], wbuf.at[slot, pl.ds(9 * k, 9)], w_sem.at[slot, k])

        def latent_copy(row):
            return pltpu.make_async_copy(latent.at[:, row], raw.at[0, row, pl.ds(2, n_frames)], lat_sem.at[row])

        def out_copy(row):
            return pltpu.make_async_copy(raw.at[0, row, pl.ds(2, n_frames)], out.at[:, row], out_sem.at[row])

        def halo_copy(layer, slot, row):
            return pltpu.make_async_remote_copy(
                src_ref=raw.at[slot, row, pl.ds(2, n_frames)], dst_ref=raw.at[slot, row, pl.ds(0, n_frames)],
                send_sem=halo_send.at[layer, row], recv_sem=halo_recv.at[layer, row],
                device_id={"cp": me + 1}, device_id_type=MESH)

        def stat_copy(layer, hop):
            return pltpu.make_async_remote_copy(
                src_ref=stat.at[layer, me], dst_ref=stat.at[layer, me],
                send_sem=st_send.at[layer, hop - 1], recv_sem=st_recv.at[layer, hop - 1],
                device_id={"cp": lax.rem(me + hop, n_ranks)}, device_id_type=MESH)

        def send_stats(layer):
            stat[layer, me, 0:1, :] = jnp.sum(sums[0], axis=0, keepdims=True)
            stat[layer, me, 1:2, :] = jnp.sum(sums[1], axis=0, keepdims=True)
            for hop in range(1, n_ranks):
                stat_copy(layer, hop).start()

        def add_sums(val, cols):
            slabs = val.reshape(n_cols // 8, 8, val.shape[-1])
            sums[0, :, cols] += jnp.sum(slabs, axis=0)
            sums[1, :, cols] += jnp.sum(slabs * slabs, axis=0)

        def body():
            for row in range(n_rows):
                latent_copy(row).start()
            for k in (2, 1, 0):
                weight_copy(0, 0, k).start()
            barrier = pltpu.get_barrier_semaphore()
            for hop in range(1, n_ranks):
                pl.semaphore_signal(barrier, inc=1, device_id={"cp": lax.rem(me + hop, n_ranks)}, device_id_type=MESH)
            sums[...] = jnp.zeros_like(sums)
            for row in range(n_rows):
                latent_copy(row).wait()
                for frame in range(n_frames):
                    for half in range(halves):
                        cols = pl.ds(half * HALF, HALF)
                        add_sums(raw[0, row, 2 + frame, :, cols].astype(jnp.float32), cols)
            pl.semaphore_wait(barrier, n_ranks - 1)
            send_stats(0)

            @pl.when(has_next)
            def _():
                for row in range(n_rows):
                    halo_copy(0, 0, row).start()

            def layer_step(layer, carry):
                slot = lax.rem(layer, 2)
                other = 1 - slot
                adds_input = slot == 1
                last = layer == N_LAYERS - 1

                @pl.when(jnp.logical_not(last))
                def _():
                    for k in (2, 1, 0):
                        weight_copy(layer + 1, other, k).start()

                sums[...] = jnp.zeros_like(sums)
                for hop in range(1, n_ranks):
                    stat_copy(layer, hop).wait_recv()
                total = stat[layer, 0]
                for rank in range(1, n_ranks):
                    total = total + stat[layer, rank]
                lane = lax.broadcasted_iota(jnp.int32, total.shape, 1)
                step = 1
                while step < width:
                    lower = pltpu.roll(total, step, 1)
                    upper = pltpu.roll(total, n_chans - step, 1)
                    total = total + jnp.where(lax.rem(lax.div(lane, step), 2) == 0, upper, lower)
                    step *= 2
                mean = total[0:1] * (1.0 / elem_count)
                var = total[1:2] * (1.0 / elem_count) - mean * mean
                scale = lax.rsqrt(var + NORM_EPS) * gammas[pl.ds(layer, 1), :]
                coef[0:1, :] = scale
                coef[1:2, :] = betas[pl.ds(layer, 1), :] - mean * scale

                def act_piece(row, frame, half):
                    cols = pl.ds(half * HALF, HALF)
                    src = jnp.where(is_first, 2, frame) if frame < 2 else frame
                    val = raw[slot, row, src, :, cols].astype(jnp.float32)
                    normed = (val * coef[0:1, cols] + coef[1:2, cols]).astype(jnp.bfloat16).astype(jnp.float32)
                    arg = 0.5 * normed
                    res = arg * jnp.tanh(arg) + arg
                    act_c[row, frame, :, cols] = res.astype(jnp.bfloat16)
                    edge = lax.broadcasted_iota(jnp.int32, (16, HALF), 0)
                    moved = pltpu.roll(res, 1, 0)
                    act_l[row, frame, 0:16, cols] = jnp.where(edge == 0, 0.0, moved[:16]).astype(jnp.bfloat16)
                    act_l[row, frame, 16:n_cols, cols] = moved[16:].astype(jnp.bfloat16)
                    moved = pltpu.roll(res, n_cols - 1, 0)
                    act_r[row, frame, 0:n_cols - 16, cols] = moved[:n_cols - 16].astype(jnp.bfloat16)
                    act_r[row, frame, n_cols - 16:n_cols, cols] = jnp.where(edge == 15, 0.0, moved[n_cols - 16:]).astype(jnp.bfloat16)

                def act_jobs(row, local):
                    frames = (2, 3) if local else (0, 1)
                    return [functools.partial(act_piece, row, frame, half) for frame in frames for half in range(halves)]

                def out_piece(row, frame, mxu):
                    cols = pl.ds(mxu * HALF, HALF)
                    got = sums_of[row][frame * n_cols:(frame + 1) * n_cols, mxu * HALF:(mxu + 1) * HALF] + biases[pl.ds(layer, 1), cols]
                    inner = got.astype(jnp.bfloat16).astype(jnp.float32)
                    held = raw[other, row, 2 + frame, :, cols].astype(jnp.float32)
                    new = jnp.where(adds_input, held + inner, inner).astype(jnp.bfloat16)
                    raw[other, row, 2 + frame, :, cols] = new
                    add_sums(new.astype(jnp.float32), cols)

                def out_jobs(row):
                    return [functools.partial(out_piece, row, frame, mxu) for frame in range(n_frames) for mxu in range(halves)]

                def finish_row(row):
                    @pl.when(jnp.logical_and(jnp.logical_not(last), has_next))
                    def _():
                        halo_copy(layer + 1, other, row).start()

                    @pl.when(last)
                    def _():
                        out_copy(row).start()

                def taps(row, ks):
                    return [(row, k, di, dj) for k in ks for dj in (-1, 0, 1) for di in (-1, 0, 1) if 0 <= row + di < n_rows]

                segments = []
                for row in range(n_rows + SKEW):
                    if row < n_rows:
                        segments.append(("new", row))
                    if row >= SKEW:
                        segments.append(("old", row - SKEW))
                seq = [taps(row, (2,) if kind == "new" else (1, 0)) for kind, row in segments]
                flat = [tile for tiles in seq for tile in tiles]

                sums_of = {}

                def tile_job(idx):
                    row, k, di, dj = flat[idx]
                    lhs = acts[dj][row + di, pl.ds(k, n_frames)].reshape(n_frames * n_cols, n_chans)
                    part = jnp.dot(lhs, wbuf[slot, 9 * k + 3 * (di + 1) + dj + 1], preferred_element_type=jnp.float32)
                    sums_of[row] = part if row not in sums_of else sums_of[row] + part

                def wait_halo(row):
                    @pl.when(jnp.logical_not(is_first))
                    def _():
                        halo_copy(layer, slot, row).wait_recv()

                weight_copy(layer, slot, 2).wait()
                for row in (0, 1):
                    for job in act_jobs(row, True):
                        job()

                done, pending, idx = 0, None, 0
                for kind, row in segments:
                    side = []
                    if kind == "new" and row + 2 < n_rows:
                        side += act_jobs(row + 2, True)
                    if kind == "new" and row in (SKEW - 1, SKEW):
                        wait_halo(row - SKEW + 1)
                        side += act_jobs(row - SKEW + 1, False)
                    if kind == "old" and row == 0:
                        weight_copy(layer, slot, 1).wait()
                        weight_copy(layer, slot, 0).wait()
                    if kind == "old" and row + 2 < n_rows:
                        wait_halo(row + 2)
                        side += act_jobs(row + 2, False)
                    if pending is not None:
                        side = out_jobs(pending) + side
                    count = len(seq[segments.index((kind, row))])
                    for job in interleave([functools.partial(tile_job, idx + j) for j in range(count)], side):
                        job()
                    idx += count
                    if pending is not None:
                        finish_row(pending)
                        pending = None
                    if kind == "old":
                        pending = row
                for job in out_jobs(pending):
                    job()

                @pl.when(jnp.logical_not(last))
                def _():
                    send_stats(layer + 1)

                finish_row(pending)

                @pl.when(has_next)
                def _():
                    for row in range(n_rows):
                        halo_copy(layer, slot, row).wait_send()

                for hop in range(1, n_ranks):
                    stat_copy(layer, hop).wait_send()
                return carry

            lax.fori_loop(0, N_LAYERS, layer_step, 0)
            for row in range(n_rows):
                out_copy(row).wait()

        body()

    return kernel


def solution(mesh):
    n_ranks = mesh.shape["cp"]
    frame_spec = P(("dp", "cp"))

    def local_fn(latent, conv_kernels, conv_biases, gn_gammas, gn_betas):
        n_frames, n_rows, n_cols, n_chans = latent.shape
        weights = conv_kernels.reshape(N_LAYERS, 27, n_chans, n_chans)
        act_shape = pltpu.VMEM((n_rows, 4, n_cols, n_chans), jnp.bfloat16)
        return pl.pallas_call(
            make_kernel(n_ranks, n_frames, n_rows, n_cols, n_chans),
            out_shape=jax.ShapeDtypeStruct(latent.shape, latent.dtype),
            in_specs=[pl.BlockSpec(memory_space=pl.ANY)] * 2 + [pl.BlockSpec(memory_space=pltpu.VMEM)] * 3,
            out_specs=pl.BlockSpec(memory_space=pl.ANY),
            scratch_shapes=[
                pltpu.VMEM((2, 27, n_chans, n_chans), jnp.bfloat16),
                act_shape, act_shape, act_shape,
                pltpu.VMEM((2, n_rows, 4, n_cols, n_chans), jnp.bfloat16),
                pltpu.VMEM((N_LAYERS, n_ranks, 2, n_chans), jnp.float32),
                pltpu.VMEM((2, 8, n_chans), jnp.float32),
                pltpu.VMEM((2, n_chans), jnp.float32),
                pltpu.SemaphoreType.DMA((2, 3)),
                pltpu.SemaphoreType.DMA((n_rows,)),
                pltpu.SemaphoreType.DMA((n_rows,)),
                pltpu.SemaphoreType.DMA((N_LAYERS, n_rows)),
                pltpu.SemaphoreType.DMA((N_LAYERS, n_rows)),
                pltpu.SemaphoreType.DMA((N_LAYERS, n_ranks - 1)),
                pltpu.SemaphoreType.DMA((N_LAYERS, n_ranks - 1)),
            ],
            compiler_params=pltpu.CompilerParams(collective_id=0, has_side_effects=True, vmem_limit_bytes=60 * 1024 * 1024),
            name="decode",
        )(latent, weights, conv_biases, gn_gammas, gn_betas)

    return jax.shard_map(local_fn, mesh=mesh, in_specs=(frame_spec, P(), P(), P(), P()), out_specs=frame_spec, check_vma=False)
```

time: 259 us -> 96.8 us (0.37); the launches traced: 254 us -> 96.6 us
  matrix products: 99.5 us -> 0 us
  Pallas kernels: 0 us -> 94.2 us
  waiting for transfers between devices: 51.6 us -> 0 us
  blocking collectives: 49.7 us -> 0 us
  local copies, waits for them, and re-layouts: 31.3 us -> 2.36 us
  starting transfers between devices: 11 us -> 0 us
  other arithmetic: 10.4 us -> 0 us
    conv_general_dilated x4 -> x0, matrix products: 99.5 us -> none  [conv_frames(): lax.conv_general_dilated(padded[None], kernel, window_strides=(1, 1, 1),...]
    pallas_call x0 -> x1, Pallas kernels: none -> 94.2 us  [local_fn(): pl.pallas_call(make_kernel(n_ranks, n_frames, n_rows, n_cols, n_chans), o...]
    ppermute x4 -> x0, waiting for transfers between devices: 51.6 us -> none  [conv_step(): from_prev = lax.ppermute(act_in[n_frames - 2:], 'cp', next_perm)]
    psum x4 -> x0, blocking collectives: 49.7 us -> none  [gn_step(): grp_sums = lax.psum(group_sums(hidden), 'cp')]
    conv_general_dilated x16 -> x0, local copies, waits for them, and re-layouts: 15.3 us -> none  [conv_frames(): lax.conv_general_dilated(padded[None], kernel, window_strides=(1, 1, 1),...]
    ppermute x4 -> x0, starting transfers between devices: 11 us -> none  [conv_step(): from_prev = lax.ppermute(act_in[n_frames - 2:], 'cp', next_perm)]
    convert_element_type x5 -> x0, other arithmetic: 5.64 us -> none  [the longest x4 4.12 us: norm_act(): return jax.nn.silu(normed.astype(jnp.float32)).astype(jnp.bfloat16)]
    unnamed x12 -> x1, local copies, waits for them, and re-layouts: 7.82 us -> 2.36 us
  transfers between devices with their start and end apart: 4 -> 0, of which waited for: 4 -> 0; matrix products, arithmetic and copies ran while one was open for 0% -> 0% of each run, Pallas kernels for 0% -> 0%
where the time goes in v1:
time: 96.8 us; the launch traced here: 96.6 us
  Pallas kernels  94.2 us (97%)
  local copies, waits for them, and re-layouts  2.36 us (2%)
    pallas_call x1, Pallas kernels, local_fn(): pl.pallas_call(make_kernel(n_ranks, n_frames, n_rows, n_cols, n_chans), o...  94.2 us
    unnamed x1, local copies, waits for them, and re-layouts  2.36 us

profile of v1, /device:TPU:81, one launch (start us, length us, event | category | flops | bytes accessed | tf_op | source)
XLA Modules:
  0.0 96.6 jit_solution(7684727576854694467)
XLA Ops:
  0.0 94.2 %decode.1 = bf16[2,6,96,512]{3,2,1,0:T(8,128)(2,1)} custom-call(bf16[2,6,96,512]{3,2,1,0:T(8,128)(2,1)} %latent.1, bf16[4,27,512,512]{3,2,1,0:T(8,128)(2,1)} %bitcast.1, f32[4,512]{1,0:T(4,128)} %biases.1, f32[4,512]{1,0:T(4,128)} %gammas.1, f32[4,512]{1,0:T(4,128)} %betas.1), custom_call_target="tpu_custom_call" | custom-call | tf_op jit(solution)/shard_map/decode/pallas_call | solution.py:259
  94.2 2.4 %copy.7 = bf16[2,6,96,512]{3,2,1,0:T(8,128)(2,1)} copy(bf16[2,6,96,512]{3,2,1,0:T(8,128)(2,1)} %decode.1) | data formatting | bytes 2359296

commit v2 on v0

v2 whole, which is shorter than its diff:
```python
import functools

import jax
import jax.numpy as jnp
from jax import lax
from jax.experimental import pallas as pl
from jax.experimental.pallas import tpu as pltpu
from jax.sharding import PartitionSpec as P

GROUPS = 32
NORM_EPS = 1e-6
N_LAYERS = 4
HALF = 256
MESH = pl.DeviceIdType.MESH


def interleave(long, short):
    if not short:
        return list(long)
    out, taken = [], 0
    for idx, job in enumerate(long):
        due = (idx * len(short)) // max(len(long), 1) + 1
        while taken < min(due, len(short)):
            out.append(short[taken])
            taken += 1
        out.append(job)
    return out + list(short[taken:])


def make_kernel(n_ranks, n_frames, n_rows, n_cols, n_chans):
    width = n_chans // GROUPS
    elem_count = float(n_ranks * n_frames * n_rows * n_cols * width)
    halves = n_chans // HALF
    pairs = [((row,), (row + 1,)) for row in range(1, n_rows - 1, 2)] + [((0,), (n_rows - 1,))]
    block = n_frames * n_cols

    def kernel(latent, weights, biases, gammas, betas, out, wbuf, act_0l, act_0c, act_0r, act_1l, act_1c, act_1r, raw, part, stat,
               sums, coef, w_sem, lat_sem, halo_send, halo_recv, st_send, st_recv):
        acts = ({-1: act_0l, 0: act_0c, 1: act_0r}, {-1: act_1l, 0: act_1c, 1: act_1r})
        me = lax.axis_index("cp")
        is_first = me == 0
        nought = lax.rem(me * (me + 1), 2)

        def weight_copy(layer, slot, k):
            return pltpu.make_async_copy(weights.at[layer, pl.ds(9 * k, 9)], wbuf.at[slot, pl.ds(9 * k, 9)], w_sem.at[slot, k])

        def latent_copy(half, row):
            return pltpu.make_async_copy(latent.at[:, row, :, pl.ds(half * HALF, HALF)],
                                         raw.at[0, half, row, pl.ds(2, n_frames)], lat_sem.at[half, row])

        def out_copy(half, row):
            return pltpu.make_async_copy(raw.at[0, half, row, pl.ds(2, n_frames)],
                                         out.at[:, row, :, pl.ds(half * HALF, HALF)], lat_sem.at[half, row])

        def halo_copy(layer, slot, half, row):
            return pltpu.make_async_remote_copy(
                src_ref=raw.at[slot, half, row, pl.ds(2, n_frames)], dst_ref=raw.at[slot, half, row, pl.ds(0, n_frames)],
                send_sem=halo_send.at[slot, half, row], recv_sem=halo_recv.at[slot, half, row],
                device_id={"cp": lax.rem(me + 1, n_ranks)}, device_id_type=MESH)

        def stat_copy(layer, half, hop):
            turn = layer % 2 if isinstance(layer, int) else lax.rem(layer, 2)
            return pltpu.make_async_remote_copy(
                src_ref=stat.at[layer, half, me], dst_ref=stat.at[layer, half, me],
                send_sem=st_send.at[turn, half, hop - 1], recv_sem=st_recv.at[turn, half, hop - 1],
                device_id={"cp": lax.rem(me + hop, n_ranks)}, device_id_type=MESH)

        def send_stats(layer, half):
            stat[layer, half, me, 0:1, :] = jnp.sum(sums[half, 0], axis=0, keepdims=True)
            stat[layer, half, me, 1:2, :] = jnp.sum(sums[half, 1], axis=0, keepdims=True)
            for hop in range(1, n_ranks):
                stat_copy(layer, half, hop).start()

        def clear_sums(half):
            sums[half] = jnp.zeros(sums.shape[1:], sums.dtype)

        def add_sums(val, half):
            slabs = val.reshape(n_cols // 8, 8, val.shape[-1])
            sums[half, 0] += jnp.sum(slabs, axis=0)
            sums[half, 1] += jnp.sum(slabs * slabs, axis=0)

        def take_stats(layer, param, half):
            for hop in range(1, n_ranks):
                stat_copy(layer, half, hop).wait_recv()
            total = stat[layer, half, 0]
            for rank in range(1, n_ranks):
                total = total + stat[layer, half, rank]
            lane = lax.broadcasted_iota(jnp.int32, total.shape, 1)
            step = 1
            while step < width:
                lower = pltpu.roll(total, step, 1)
                upper = pltpu.roll(total, HALF - step, 1)
                total = total + jnp.where(lax.rem(lax.div(lane, step), 2) == 0, upper, lower)
                step *= 2
            cols = pl.ds(half * HALF, HALF)
            mean = total[0:1] * (1.0 / elem_count)
            var = total[1:2] * (1.0 / elem_count) - mean * mean
            scale = lax.rsqrt(var + NORM_EPS) * gammas[pl.ds(param, 1), cols]
            coef[half, 0:1, :] = scale
            coef[half, 1:2, :] = betas[pl.ds(param, 1), cols] - mean * scale

        def act_piece(slot, half, row, frame):
            left, centre, right = acts[half][-1], acts[half][0], acts[half][1]
            src = jnp.where(is_first, 2, frame) if frame < 2 else frame
            val = raw[slot, half, row, src].astype(jnp.float32)
            normed = (val * coef[half, 0:1] + coef[half, 1:2]).astype(jnp.bfloat16).astype(jnp.float32)
            arg = 0.5 * normed
            res = arg * jnp.tanh(arg) + arg
            centre[row, frame] = res.astype(jnp.bfloat16)
            edge = lax.broadcasted_iota(jnp.int32, (16, HALF), 0)
            moved = pltpu.roll(res, 1, 0)
            left[row, frame, 0:16] = jnp.where(edge == 0, 0.0, moved[:16]).astype(jnp.bfloat16)
            left[row, frame, 16:n_cols] = moved[16:].astype(jnp.bfloat16)
            moved = pltpu.roll(res, n_cols - 1, 0)
            right[row, frame, 0:n_cols - 16] = moved[:n_cols - 16].astype(jnp.bfloat16)
            right[row, frame, n_cols - 16:n_cols] = jnp.where(edge == 15, 0.0, moved[n_cols - 16:]).astype(jnp.bfloat16)

        def act_jobs(slot, half, row, local):
            return [functools.partial(act_piece, slot, half, row, frame) for frame in ((2, 3) if local else (0, 1))]

        for half in range(halves):
            for row in range(n_rows):
                latent_copy(half, row).start()
        for k in (2, 1, 0):
            weight_copy(0, 0, k).start()
        barrier = pltpu.get_barrier_semaphore()
        for hop in range(1, n_ranks):
            pl.semaphore_signal(barrier, inc=1, device_id={"cp": lax.rem(me + hop, n_ranks)}, device_id_type=MESH)
        for half in range(halves):
            clear_sums(half)
            for row in range(n_rows):
                latent_copy(half, row).wait()
                for frame in range(n_frames):
                    add_sums(raw[0, half, row, 2 + frame].astype(jnp.float32), half)
        pl.semaphore_wait(barrier, n_ranks - 1)
        for half in range(halves):
            send_stats(0, half)
        for half in range(halves):
            for row in range(n_rows):
                halo_copy(0, 0, half, row).start()
        take_stats(0, 0, 0)
        for row in range(2):
            for job in act_jobs(0, 0, row, True):
                job()

        def layer_step(layer, carry):
            slot = lax.rem(layer, 2)
            other = 1 - slot
            adds_input = slot == 1
            last = layer == N_LAYERS - 1

            @pl.when(jnp.logical_not(last))
            def _():
                for k in (2, 1, 0):
                    weight_copy(layer + 1, other, k).start()

            vals = {}

            def accumulate(key, lhs, tap, in_half, cols, where=None):
                term = jnp.dot(lhs, wbuf[slot if where is None else where, tap, pl.ds(in_half * HALF, HALF), cols], preferred_element_type=jnp.float32)
                vals[key] = term if key not in vals else vals[key] + term

            def taps(k):
                return [(di, dj, 9 * k + 3 * (di + 1) + dj + 1) for dj in (-1, 0, 1) for di in (0, 1, -1)]

            def row_tile(key, row, k, di, dj, tap, in_half):
                lhs = acts[in_half][dj][row + di, pl.ds(k, n_frames)].reshape(block, HALF)
                accumulate(key, lhs, tap, in_half, pl.ds(0, n_chans))

            def row_chain(key, row, k, in_half):
                return [functools.partial(row_tile, key, row, k, di, dj, tap, in_half)
                        for di, dj, tap in taps(k) if 0 <= row + di < n_rows]

            def set_tile(tag, rows, di, dj, tap, in_half, out_half):
                inside = [row for row in rows if 0 <= row + di < n_rows]
                count = len(inside)
                lhs = acts[in_half][dj][pl.ds(inside[0] + di, count), pl.ds(tap // 9, n_frames)].reshape(count * block, HALF)
                accumulate((tag, rows), lhs, tap, in_half, pl.ds(out_half * HALF, HALF))

            def pair_chain(tag, pair, k, in_half, out_half):
                streams = [[functools.partial(set_tile, tag, rows, di, dj, tap, in_half, out_half) for di, dj, tap in taps(k)
                            if any(0 <= row + di < n_rows for row in rows)] for rows in pair]
                return [job for jobs in zip(*streams) for job in jobs]

            def keep_piece(key, row, frame, first, cols):
                span = slice(frame * n_cols, (frame + 1) * n_cols)
                got = vals[key][span]
                part[row, span, cols] = got if first else part[row, span, cols] + got

            def keep_jobs(key, row, first, half=None):
                cols = pl.ds(0, n_chans) if half is None else pl.ds(half * HALF, HALF)
                return [functools.partial(keep_piece, key, row, frame, first, cols) for frame in range(n_frames)]

            def out_piece(tag, rows, row, half, frame):
                span = slice(frame * n_cols, (frame + 1) * n_cols)
                base = (row - rows[0]) * block + frame * n_cols
                cols = pl.ds(half * HALF, HALF)
                got = jnp.where(nought == 0, vals[tag, rows][base:base + n_cols], 0.0) + part[row, span, cols] + biases[pl.ds(layer, 1), cols]
                inner = got.astype(jnp.bfloat16).astype(jnp.float32)
                held = raw[other, half, row, 2 + frame].astype(jnp.float32)
                new = jnp.where(adds_input, held + inner, inner).astype(jnp.bfloat16)
                raw[other, half, row, 2 + frame] = new
                add_sums(new.astype(jnp.float32), half)

            def out_jobs(tag, pair, half):
                return [functools.partial(out_piece, tag, rows, row, half, frame)
                        for rows in pair for row in rows for frame in range(n_frames)]

            def send_jobs(half, rows):
                return [lambda row=row: halo_copy(layer + 1, other, half, row).start() for row in rows]

            def halo_jobs(half, row):
                return [lambda: halo_copy(layer, slot, half, row).wait_recv()] + act_jobs(slot, half, row, False)

            def run(tiles, side=()):
                for job in interleave(tiles, list(side)):
                    job()

            later = []
            spread = [[(0, 1)], [(2,)], [(3,)], [(4,)], [(5,)]]
            for k in (2, 1, 0):
                weight_copy(layer, slot, k).wait()
                for row in range(n_rows):
                    key = ("row", k, row)
                    side = later
                    if k == 2 and row + 2 < n_rows:
                        side = side + act_jobs(slot, 0, row + 2, True)
                    if k == 2 and row >= n_rows - 2:
                        side = side + halo_jobs(0, row - n_rows + 2)
                    if k == 1 and row + 2 < n_rows:
                        side = side + halo_jobs(0, row + 2)
                    if k == 0 and row == 1:
                        side = side + [functools.partial(take_stats, layer, layer, 1)]
                    if k == 0 and row >= 1:
                        side = side + [job for rows in spread[row - 1] for got in rows for job in act_jobs(slot, 1, got, True)]
                    run(row_chain(key, row, k, 0), side)
                    later = keep_jobs(key, row, k == 2)

            clear_sums(0)
            for idx, pair in enumerate(pairs):
                tag = ("first", idx)
                ready = [(0, 1, 2, 3), (4, 5), ()][idx]
                run(pair_chain(tag, pair, 2, 1, 0), [job for row in ready for job in halo_jobs(1, row)])
                run(pair_chain(tag, pair, 1, 1, 0) + pair_chain(tag, pair, 0, 1, 0), later)
                later = out_jobs(tag, pair, 0) + (send_jobs(0, (1, 2)) if idx == 0 else [])

            later = later + [functools.partial(send_stats, layer + 1, 0), functools.partial(clear_sums, 1)]
            later = later + send_jobs(0, (0, 3, 4, 5))
            for idx, pair in enumerate(pairs):
                tag = ("second", idx)
                early = later if idx == 0 else []
                run(pair_chain(tag, pair, 2, 1, 1), early)
                run(pair_chain(tag, pair, 1, 1, 1) + pair_chain(tag, pair, 0, 1, 1), [] if idx == 0 else later)
                later = out_jobs(tag, pair, 1)
            for job in later:
                job()

            @pl.when(jnp.logical_not(last))
            def _():
                send_stats(layer + 1, 1)

            @pl.when(jnp.logical_not(last))
            def _():
                for row in range(n_rows):
                    halo_copy(layer + 1, other, 1, row).start()

            @pl.when(last)
            def _():
                for half in range(halves):
                    for row in range(n_rows):
                        out_copy(half, row).start()

            take_stats(layer + 1, jnp.minimum(layer + 1, N_LAYERS - 1), 0)
            for row in range(2):
                for job in act_jobs(other, 0, row, True):
                    job()

            for half in range(halves):
                for row in range(n_rows):
                    halo_copy(layer, slot, half, row).wait_send()
                for hop in range(1, n_ranks):
                    stat_copy(layer, half, hop).wait_send()
            return carry

        lax.fori_loop(0, N_LAYERS, layer_step, 0)
        for hop in range(1, n_ranks):
            stat_copy(N_LAYERS, 0, hop).wait_send()
        for row in range(n_rows):
            halo_copy(N_LAYERS, 0, 0, row).wait_send()
            halo_copy(N_LAYERS, 0, 0, row).wait_recv()
        for half in range(halves):
            for row in range(n_rows):
                out_copy(half, row).wait()

    return kernel


def solution(mesh):
    n_ranks = mesh.shape["cp"]
    frame_spec = P(("dp", "cp"))

    def local_fn(latent, conv_kernels, conv_biases, gn_gammas, gn_betas):
        n_frames, n_rows, n_cols, n_chans = latent.shape
        weights = conv_kernels.reshape(N_LAYERS, 27, n_chans, n_chans)
        halves = n_chans // HALF
        act_shape = pltpu.VMEM((n_rows, 4, n_cols, HALF), jnp.bfloat16)
        return pl.pallas_call(
            make_kernel(n_ranks, n_frames, n_rows, n_cols, n_chans),
            out_shape=jax.ShapeDtypeStruct(latent.shape, latent.dtype),
            in_specs=[pl.BlockSpec(memory_space=pl.ANY)] * 2 + [pl.BlockSpec(memory_space=pltpu.VMEM)] * 3,
            out_specs=pl.BlockSpec(memory_space=pl.ANY),
            scratch_shapes=[
                pltpu.VMEM((2, 27, n_chans, n_chans), jnp.bfloat16),
                act_shape, act_shape, act_shape, act_shape, act_shape, act_shape,
                pltpu.VMEM((2, halves, n_rows, 4, n_cols, HALF), jnp.bfloat16),
                pltpu.VMEM((n_rows, n_frames * n_cols, n_chans), jnp.float32),
                pltpu.VMEM((N_LAYERS + 1, halves, n_ranks, 2, HALF), jnp.float32),
                pltpu.VMEM((halves, 2, 8, HALF), jnp.float32),
                pltpu.VMEM((halves, 2, HALF), jnp.float32),
                pltpu.SemaphoreType.DMA((2, 3)),
                pltpu.SemaphoreType.DMA((halves, n_rows)),
                pltpu.SemaphoreType.DMA((2, halves, n_rows)),
                pltpu.SemaphoreType.DMA((2, halves, n_rows)),
                pltpu.SemaphoreType.DMA((2, halves, n_ranks - 1)),
                pltpu.SemaphoreType.DMA((2, halves, n_ranks - 1)),
            ],
            compiler_params=pltpu.CompilerParams(collective_id=0, has_side_effects=True, vmem_limit_bytes=60 * 1024 * 1024),
            name="decode",
        )(latent, weights, conv_biases, gn_gammas, gn_betas)

    return jax.shard_map(local_fn, mesh=mesh, in_specs=(frame_spec, P(), P(), P(), P()), out_specs=frame_spec, check_vma=False)
```

time: 259 us -> 87.7 us (0.34); the launches traced: 254 us -> 86.2 us
  matrix products: 99.5 us -> 0 us
  Pallas kernels: 0 us -> 83.9 us
  waiting for transfers between devices: 51.6 us -> 0 us
  blocking collectives: 49.7 us -> 0 us
  local copies, waits for them, and re-layouts: 31.3 us -> 2.36 us
  starting transfers between devices: 11 us -> 0 us
  other arithmetic: 10.4 us -> 0 us
    conv_general_dilated x4 -> x0, matrix products: 99.5 us -> none  [conv_frames(): lax.conv_general_dilated(padded[None], kernel, window_strides=(1, 1, 1),...]
    pallas_call x0 -> x1, Pallas kernels: none -> 83.9 us  [local_fn(): pl.pallas_call(make_kernel(n_ranks, n_frames, n_rows, n_cols, n_chans), o...]
    ppermute x4 -> x0, waiting for transfers between devices: 51.6 us -> none  [conv_step(): from_prev = lax.ppermute(act_in[n_frames - 2:], 'cp', next_perm)]
    psum x4 -> x0, blocking collectives: 49.7 us -> none  [gn_step(): grp_sums = lax.psum(group_sums(hidden), 'cp')]
    conv_general_dilated x16 -> x0, local copies, waits for them, and re-layouts: 15.3 us -> none  [conv_frames(): lax.conv_general_dilated(padded[None], kernel, window_strides=(1, 1, 1),...]
    ppermute x4 -> x0, starting transfers between devices: 11 us -> none  [conv_step(): from_prev = lax.ppermute(act_in[n_frames - 2:], 'cp', next_perm)]
    convert_element_type x5 -> x0, other arithmetic: 5.64 us -> none  [the longest x4 4.12 us: norm_act(): return jax.nn.silu(normed.astype(jnp.float32)).astype(jnp.bfloat16)]
    unnamed x12 -> x1, local copies, waits for them, and re-layouts: 7.82 us -> 2.36 us
  transfers between devices with their start and end apart: 4 -> 0, of which waited for: 4 -> 0; matrix products, arithmetic and copies ran while one was open for 0% -> 0% of each run, Pallas kernels for 0% -> 0%
where the time goes in v2:
time: 87.7 us; the launch traced here: 86.2 us
  Pallas kernels  83.9 us (96%)
  local copies, waits for them, and re-layouts  2.36 us (3%)
    pallas_call x1, Pallas kernels, local_fn(): pl.pallas_call(make_kernel(n_ranks, n_frames, n_rows, n_cols, n_chans), o...  83.9 us
    unnamed x1, local copies, waits for them, and re-layouts  2.36 us

profile of v2, /device:TPU:81, one launch (start us, length us, event | category | flops | bytes accessed | tf_op | source)
XLA Modules:
  0.0 86.2 jit_solution(17542746977371714426)
XLA Ops:
  0.0 83.9 %decode.1 = bf16[2,6,96,512]{3,2,1,0:T(8,128)(2,1)} custom-call(bf16[2,6,96,512]{3,2,1,0:T(8,128)(2,1)} %latent.1, bf16[4,27,512,512]{3,2,1,0:T(8,128)(2,1)} %bitcast.1, f32[4,512]{1,0:T(4,128)} %biases.1, f32[4,512]{1,0:T(4,128)} %gammas.1, f32[4,512]{1,0:T(4,128)} %betas.1), custom_call_target="tpu_custom_call" | custom-call | tf_op jit(solution)/shard_map/decode/pallas_call | solution.py:307
  83.9 2.4 %copy.7 = bf16[2,6,96,512]{3,2,1,0:T(8,128)(2,1)} copy(bf16[2,6,96,512]{3,2,1,0:T(8,128)(2,1)} %decode.1) | data formatting | bytes 2359296

commit v3 on v2

--- a/solution.py
+++ b/solution.py
@@ -216,6 +216,9 @@
                 for job in interleave(tiles, list(side)):
                     job()
 
+            def sent(row):
+                halo_copy(layer, slot, 0, row).wait_send()
+
             later = []
             spread = [[(0, 1)], [(2,)], [(3,)], [(4,)], [(5,)]]
             for k in (2, 1, 0):
@@ -232,7 +235,8 @@
                     if k == 0 and row == 1:
                         side = side + [functools.partial(take_stats, layer, layer, 1)]
                     if k == 0 and row >= 1:
-                        side = side + [job for rows in spread[row - 1] for got in rows for job in act_jobs(slot, 1, got, True)]
+                        for got in (rows for group in spread[row - 1] for rows in group):
+                            side = side + act_jobs(slot, 1, got, True) + [functools.partial(sent, got)]
                     run(row_chain(key, row, k, 0), side)
                     later = keep_jobs(key, row, k == 2)
 
@@ -241,8 +245,12 @@
                 tag = ("first", idx)
                 ready = [(0, 1, 2, 3), (4, 5), ()][idx]
                 run(pair_chain(tag, pair, 2, 1, 0), [job for row in ready for job in halo_jobs(1, row)])
-                run(pair_chain(tag, pair, 1, 1, 0) + pair_chain(tag, pair, 0, 1, 0), later)
+                run(pair_chain(tag, pair, 1, 1, 0), later)
+                run(pair_chain(tag, pair, 0, 1, 0))
                 later = out_jobs(tag, pair, 0) + (send_jobs(0, (1, 2)) if idx == 0 else [])
+
+            ahead = [functools.partial(take_stats, layer + 1, jnp.minimum(layer + 1, N_LAYERS - 1), 0)]
+            ahead = ahead + [job for row in range(2) for job in act_jobs(other, 0, row, True)]
 
             later = later + [functools.partial(send_stats, layer + 1, 0), functools.partial(clear_sums, 1)]
             later = later + send_jobs(0, (0, 3, 4, 5))
@@ -250,7 +258,10 @@
                 tag = ("second", idx)
                 early = later if idx == 0 else []
                 run(pair_chain(tag, pair, 2, 1, 1), early)
-                run(pair_chain(tag, pair, 1, 1, 1) + pair_chain(tag, pair, 0, 1, 1), [] if idx == 0 else later)
+                tiles = pair_chain(tag, pair, 1, 1, 1) + pair_chain(tag, pair, 0, 1, 1)
+                cut = len(tiles) * 3 // 4 if idx == len(pairs) - 1 else len(tiles)
+                run(tiles[:cut], [] if idx == 0 else later)
+                run(tiles[cut:], ahead if cut < len(tiles) else [])
                 later = out_jobs(tag, pair, 1)
             for job in later:
                 job()
@@ -270,13 +281,8 @@
                     for row in range(n_rows):
                         out_copy(half, row).start()
 
-            take_stats(layer + 1, jnp.minimum(layer + 1, N_LAYERS - 1), 0)
-            for row in range(2):
-                for job in act_jobs(other, 0, row, True):
-                    job()
-
             for half in range(halves):
-                for row in range(n_rows):
+                for row in range(n_rows if half else 0):
                     halo_copy(layer, slot, half, row).wait_send()
                 for hop in range(1, n_ranks):
                     stat_copy(layer, half, hop).wait_send()

time: 87.7 us -> 87.2 us (level)
  no operation moved by 1% of the time
where the time goes in v3:
time: 87.2 us; the launch traced here: 86.1 us
  Pallas kernels  83.8 us (96%)
  local copies, waits for them, and re-layouts  2.36 us (3%)
    pallas_call x1, Pallas kernels, local_fn(): pl.pallas_call(make_kernel(n_ranks, n_frames, n_rows, n_cols, n_chans), o...  83.8 us
    unnamed x1, local copies, waits for them, and re-layouts  2.36 us

profile of v3, /device:TPU:81, one launch (start us, length us, event | category | flops | bytes accessed | tf_op | source)
XLA Modules:
  0.0 86.1 jit_solution(10440791523882834549)
XLA Ops:
  0.0 83.8 %decode.1 = bf16[2,6,96,512]{3,2,1,0:T(8,128)(2,1)} custom-call(bf16[2,6,96,512]{3,2,1,0:T(8,128)(2,1)} %latent.1, bf16[4,27,512,512]{3,2,1,0:T(8,128)(2,1)} %bitcast.1, f32[4,512]{1,0:T(4,128)} %biases.1, f32[4,512]{1,0:T(4,128)} %gammas.1, f32[4,512]{1,0:T(4,128)} %betas.1), custom_call_target="tpu_custom_call" | custom-call | tf_op jit(solution)/shard_map/decode/pallas_call | solution.py:313
  83.8 2.4 %copy.7 = bf16[2,6,96,512]{3,2,1,0:T(8,128)(2,1)} copy(bf16[2,6,96,512]{3,2,1,0:T(8,128)(2,1)} %decode.1) | data formatting | bytes 2359296
